TPU v7x, 32 devices: a whole 2x2x4 slice. The times are simulated.
32 devices in a mesh: group: 2 (over y), seq: 4 (over z), tensor: 4 (over x, core).
Axes of the slice: x: 2, y: 2, z: 4, core: 2. Of those that a mesh axis runs over, the one named last changes fastest.
Arguments:
- query: bfloat16 [16, 7168], P(('group', 'seq'), 'tensor'), parts along dimension 0, may hold values from -5 to 5
- key_cache: bfloat16 [32, 256, 7168], P(('group', 'seq'), None, 'tensor'), parts along dimension 0, may hold values from -5 to 5
- value_cache: bfloat16 [32, 256, 7168], P(('group', 'seq'), None, 'tensor'), parts along dimension 0, may hold values from -6 to 6
- alibi_slopes: float32 [56], P('tensor'), may hold values from 0 to 1, as said below
- block_seq: int32 [32], P(('group', 'seq')), parts along dimension 0, may hold values from 0 to 7, as said below
- block_pos: int32 [32], P(('group', 'seq')), parts along dimension 0, may hold values from 0 to 2, as said below
- lengths: int32 [16], P('group'), parts along dimension 0, may hold values from 1 to 768, as said below
- out_weight: bfloat16 [7168, 14336], P('tensor', 'seq'), may hold values from -0.5 to 0.5
Outputs:
- mixed: bfloat16 [16, 14336], P(('group', 'tensor'), 'seq'), parts along dimension 0
There are 2 independent parts, one for each index of `group`. A program takes and returns all parts, laid end to end along the dimension named above; an argument that names none is the same for every part. Nothing has to cross between parts.
Inputs may be any that keep to these rules, and one draw needn't show every extreme that they name: `block_seq`: every sequence owns at least one block and at most 3; the blocks of sequence s have block_pos 0 to n_s - 1, each once. block_pos of a block is below the number of blocks its sequence owns. `lengths`: A sequence that owns n blocks has a length above 256 * (n - 1) and at most 256 * n. `alibi_slopes`: positive slopes.
All inputs are finite; a program needn't handle non-finite values.
Results may differ from a plain program's by a relative error of at most 0.0054.
Values may be sent and summed in bfloat16 or wider, within the bound.
No kernel may reach another device: no remote copies, remote signals or barrier semaphores. Data moves between devices by JAX's collectives and lax.ppermute only.
A program may use at most 64 MiB of HBM per device.

v0:
```python
import math
import jax
import jax.numpy as jnp
from jax import lax
from jax.sharding import PartitionSpec as P


def local(query, key_cache, value_cache, alibi_slopes, block_seq, block_pos, lengths, out_weight):
    heads = alibi_slopes.shape[0]
    features = query.shape[1]
    head_size = features // heads
    blocks_here = key_cache.shape[0]
    block_len = key_cache.shape[1]
    seq_count = lengths.shape[0]
    scale = 1.0 / math.sqrt(head_size)
    whole_query = lax.all_gather(query, "seq", axis=0, tiled=True)
    query_rows = jnp.take(whole_query, block_seq, axis=0).reshape(blocks_here, heads, head_size)
    keys = key_cache.reshape(blocks_here, block_len, heads, head_size)
    values = value_cache.reshape(blocks_here, block_len, heads, head_size)
    scores = (
        jnp.einsum("bthd,bhd->bht", keys, query_rows, preferred_element_type=jnp.float32) * scale
    )
    owner_length = lengths[block_seq]
    placed = block_pos[:, None] * block_len + jnp.arange(block_len, dtype=jnp.int32)[None, :]
    live = (placed < owner_length[:, None])[:, None, :]
    distance = (owner_length[:, None] - 1 - placed).astype(jnp.float32)
    scores = scores - alibi_slopes[None, :, None] * distance[:, None, :]
    scores = jnp.where(live, scores, -1e30)
    block_top = jnp.max(scores, axis=2)
    weights = jnp.where(live, jnp.exp(scores - block_top[:, :, None]), 0.0)
    block_total = jnp.sum(weights, axis=2)
    block_acc = jnp.einsum(
        "bht,bthd->bhd", weights.astype(jnp.bfloat16), values, preferred_element_type=jnp.float32
    )
    seq_ids = jnp.arange(seq_count, dtype=jnp.int32)
    owned = (block_seq[None, :] == seq_ids[:, None])[:, :, None]
    local_top = jnp.max(jnp.where(owned, block_top[None], -1e30), axis=1)
    factor = jnp.where(owned, jnp.exp(block_top[None] - local_top[:, None, :]), 0.0)
    local_total = jnp.sum(factor * block_total[None], axis=1)
    local_acc = jnp.einsum("sbh,bhd->shd", factor, block_acc, precision=lax.Precision.HIGHEST)
    tops, totals, accs = (
        lax.all_to_all(local_top[None], "seq", split_axis=1, concat_axis=0, tiled=True),
        lax.all_to_all(local_total[None], "seq", split_axis=1, concat_axis=0, tiled=True),
        lax.all_to_all(local_acc[None], "seq", split_axis=1, concat_axis=0, tiled=True),
    )
    best = jnp.max(tops, axis=0)
    scaling = jnp.exp(tops - best[None])
    home_total = jnp.sum(totals * scaling, axis=0)
    home_acc = jnp.sum(accs * scaling[..., None], axis=0)
    mine = (
        (home_acc / home_total[:, :, None])
        .astype(jnp.bfloat16)
        .reshape(home_acc.shape[0], features)
    )
    attention = lax.all_gather(mine, "seq", axis=0, tiled=True)
    mixed = lax.psum_scatter(
        jnp.dot(attention, out_weight, preferred_element_type=jnp.float32),
        "tensor",
        scatter_dimension=0,
        tiled=True,
    )
    return mixed.astype(jnp.bfloat16)


def solution(mesh):
    placed = (
        P(("group", "seq"), "tensor"),
        P(("group", "seq"), None, "tensor"),
        P(("group", "seq"), None, "tensor"),
        P("tensor"),
        P(("group", "seq")),
        P(("group", "seq")),
        P("group"),
        P("tensor", "seq"),
    )
    return jax.shard_map(
        local, mesh=mesh, in_specs=placed, out_specs=P(("group", "tensor"), "seq"), check_vma=False
    )
```

profile of v0, /device:TPU:0, one launch (start us, length us, event | category | flops | bytes accessed | tf_op | source)
XLA Modules:
  0.0 95.4 jit_solution(14486349411866468453)
XLA Ops:
  0.0 0.0 copy-start
  0.0 0.7 compare_select_fusion
  0.7 0.7 compare_and_fusion
  1.3 0.7 iota_compare_fusion
  2.1 0.0 copy-done
  2.1 0.6 gather_fusion
  2.7 0.7 broadcast_add_fusion
  3.4 0.1 fusion.16
  3.5 0.1 subtract_convert_fusion
  3.5 15.1 %all-gather = bf16[4,2,1792]{2,1,0:T(2,128)(2,1)S(1)} all-gather(bf16[1,2,1792]{2,1,0:T(2,128)(2,1)} %bitcast.41), channel_id=1, replica_groups=mesh['group'=2,'seq'=4,'tensor'=4] {'seq'}, dimensions={0}, use_global_device_ids=true | all-gather | bytes 35840 | tf_op jit(solution)/shard_map/all_gather | solution.py:16
  18.6 0.6 gather_fusion.1
  19.2 6.0 %copy.49 = bf16[4,256,1792]{1,2,0:T(8,128)(2,1)} copy(bf16[4,256,1792]{2,1,0:T(8,128)(2,1)} %param.9) | data formatting | bytes 7340032 | tf_op args[1]
  25.2 0.0 copy-start.1
  25.2 0.1 select_bitcast_fusion
  25.3 2.6 %fusion.9 = f32[4,14,1,256]{3,2,1,0:T(1,128)S(1)} fusion(bf16[4,256,14,128]{1,3,2,0:T(8,128)(2,1)} %bitcast.33, bf16[4,14,128,1]{2,1,0,3:T(8,128)(2,1)S(1)} %select_bitcast_fusion), kind=kOutput, calls=%fused_computation.16 | convolution fusion | flops 3670016 | bytes 3741696 | tf_op jit(solution)/shard_map/bthd,bhd->bht/dot_general | solution.py:21
  27.9 0.0 copy-done.1
  27.9 0.2 fusion.18
  28.0 0.1 select_reduce_fusion
  28.1 0.7 copy.54
  28.8 4.7 %all-to-all-start.1 = ((f32[1,8,14]{2,0,1:T(1,128)}), f32[1,8,14]{2,0,1:T(1,128)S(1)}, u32[]{:S(2)}, u32[]{:S(2)}) async-start(f32[1,8,14]{2,0,1:T(1,128)} %copy.54), calls=%async_computation.1 | async-start | bytes 8192 | tf_op jit(solution)/shard_map/all_to_all | solution.py:42
  33.6 0.2 fusion.4
  33.7 0.1 multiply_reduce_fusion.1
  33.8 6.0 %copy.50 = bf16[4,256,1792]{1,2,0:T(8,128)(2,1)} copy(bf16[4,256,1792]{2,1,0:T(8,128)(2,1)} %param.10) | data formatting | bytes 7340032 | tf_op args[2]
  39.8 0.0 copy-start.2
  39.8 3.1 %fusion.2 = f32[4,14,1,128]{3,2,1,0:T(1,128)S(1)} fusion(bf16[4,256,14,128]{1,3,2,0:T(8,128)(2,1)} %bitcast.34, bf16[4,14,256,1]{2,0,1,3:T(4,128)(2,1)S(1)} %get-tuple-element.10), kind=kOutput, calls=%fused_computation.6 | convolution fusion | flops 3670016 | bytes 3727360 | tf_op jit(solution)/shard_map/bht,bthd->bhd/dot_general | solution.py:32
  42.9 0.4 convolution_bitcast_fusion
  43.3 0.7 copy.57
  44.0 0.0 all-to-all-done.1
  44.0 5.1 %all-to-all-start.2 = ((f32[1,8,14]{2,0,1:T(1,128)}), f32[1,8,14]{2,0,1:T(1,128)S(1)}, u32[]{:S(2)}, u32[]{:S(2)}) async-start(f32[1,8,14]{2,0,1:T(1,128)} %copy.57), calls=%async_computation.2 | async-start | bytes 8192 | tf_op jit(solution)/shard_map/all_to_all | solution.py:43
  49.1 0.7 copy.51
  49.7 0.0 copy-done.2
  49.7 0.6 dynamic-slice
  51.0 3.7 %all-to-all-done.2 = f32[1,8,14]{2,0,1:T(1,128)S(1)} async-done(((f32[1,8,14]{2,0,1:T(1,128)}), f32[1,8,14]{2,0,1:T(1,128)S(1)}, u32[]{:S(2)}, u32[]{:S(2)}) %all-to-all-start.2) | async-done | bytes 480 | tf_op jit(solution)/shard_map/all_to_all | solution.py:43
  54.6 3.3 %all-to-all-start = ((f32[1,8,14,128]{3,0,2,1:T(1,128)}), f32[1,8,14,128]{3,0,2,1:T(1,128)S(1)}, u32[]{:S(2)}, u32[]{:S(2)}) async-start(f32[1,8,14,128]{3,0,2,1:T(1,128)} %copy.51), calls=%async_computation | async-start | bytes 114688 | tf_op jit(solution)/shard_map/all_to_all | solution.py:44
  58.0 0.1 copy.55
  58.1 0.1 copy.58
  58.2 5.5 %all-to-all-done = f32[1,8,14,128]{3,0,2,1:T(1,128)S(1)} async-done(((f32[1,8,14,128]{3,0,2,1:T(1,128)}), f32[1,8,14,128]{3,0,2,1:T(1,128)S(1)}, u32[]{:S(2)}, u32[]{:S(2)}) %all-to-all-start) | async-done | bytes 57376 | tf_op jit(solution)/shard_map/all_to_all | solution.py:44
  63.6 0.1 multiply_reduce_fusion
  63.8 0.1 fusion.15
  63.9 13.2 %all-gather.1 = bf16[4,2,1792]{2,1,0:T(2,128)(2,1)S(1)} all-gather(bf16[1,2,1792]{2,1,0:T(2,128)(2,1)S(1)} %fusion.15), channel_id=1, replica_groups=mesh['group'=2,'seq'=4,'tensor'=4] {'seq'}, dimensions={0}, use_global_device_ids=true | all-gather | bytes 35840 | tf_op jit(solution)/shard_map/all_gather | solution.py:55
  77.1 6.4 %fusion.20 = f32[8,3584]{1,0:T(8,128)S(1)} fusion(bf16[8,1792]{1,0:T(8,128)(2,1)S(1)} %reshape.152, bf16[1792,3584]{1,0:T(8,128)(2,1)} %param.15), kind=kOutput, calls=%fused_computation.41 | convolution fusion | flops 102760448 | bytes 12988416 | tf_op jit(solution)/shard_map/dot_general | solution.py:57
  83.5 11.3 %all-reduce = bf16[8,3584]{1,0:T(8,128)(2,1)S(1)} all-reduce(f32[8,3584]{1,0:T(8,128)S(1)} %fusion.20), channel_id=2, replica_groups=mesh['group'=2,'seq'=4,'tensor'=4] {'tensor'}, use_global_device_ids=true, to_apply=%region_7.8.clone | all-reduce | flops 28672 | bytes 172032
  94.7 0.6 dynamic-slice_convert_fusion
  (7 shorter events, 0.1 us)
Async XLA Ops:
  0.0 2.1 %copy-start = (s32[8]{0:T(128)S(1)}, s32[8]{0:T(128)}, u32[]{:S(2)}) copy-start(s32[8]{0:T(128)} %param.14) | copy-start | bytes 100
  25.2 2.7 %copy-start.1 = (f32[14]{0:T(128)S(1)}, f32[14]{0:T(128)}, u32[]{:S(2)}) copy-start(f32[14]{0:T(128)} %param.11) | copy-start | bytes 172
  28.8 15.2 %all-to-all-start.1 = ((f32[1,8,14]{2,0,1:T(1,128)}), f32[1,8,14]{2,0,1:T(1,128)S(1)}, u32[]{:S(2)}, u32[]{:S(2)}) async-start(f32[1,8,14]{2,0,1:T(1,128)} %copy.54), calls=%async_computation.1 | async-start | bytes 8192 | tf_op jit(solution)/shard_map/all_to_all | solution.py:42
  39.8 9.9 %copy-start.2 = (u32[32]{0:T(128)S(1)}, u32[32]{0:T(128)}, u32[]{:S(2)}) copy-start(u32[32]{0:T(128)} %constant.39) | copy-start | bytes 388
  44.0 10.7 %all-to-all-start.2 = ((f32[1,8,14]{2,0,1:T(1,128)}), f32[1,8,14]{2,0,1:T(1,128)S(1)}, u32[]{:S(2)}, u32[]{:S(2)}) async-start(f32[1,8,14]{2,0,1:T(1,128)} %copy.57), calls=%async_computation.2 | async-start | bytes 8192 | tf_op jit(solution)/shard_map/all_to_all | solution.py:43
  54.6 9.0 %all-to-all-start = ((f32[1,8,14,128]{3,0,2,1:T(1,128)}), f32[1,8,14,128]{3,0,2,1:T(1,128)S(1)}, u32[]{:S(2)}, u32[]{:S(2)}) async-start(f32[1,8,14,128]{3,0,2,1:T(1,128)} %copy.51), calls=%async_computation | async-start | bytes 114688 | tf_op jit(solution)/shard_map/all_to_all | solution.py:44
where the time goes:
time: 96.1 us; the launch traced here: 95.4 us
  blocking collectives  39.5 us (41%)
  local copies, waits for them, and re-layouts  16.7 us (17%)
  starting transfers between devices  13.1 us (14%)
  matrix products  12.5 us (13%)
  waiting for transfers between devices  9.12 us (9%)
  other arithmetic  3.75 us (4%)
    all_gather x1, blocking collectives, local(): whole_query = lax.all_gather(query, 'seq', axis=0, tiled=True)  15.1 us
    all_gather x1, blocking collectives, local(): attention = lax.all_gather(mine, 'seq', axis=0, tiled=True)  13.2 us
    unnamed x11, local copies, waits for them, and re-layouts  12.6 us
    unnamed x1, blocking collectives  11.3 us
    dot_general x1, matrix products, local(): jnp.dot(attention, out_weight, preferred_element_type=jnp.float32)  6.41 us
    all_to_all x1, waiting for transfers between devices, local(): lax.all_to_all(local_acc[None], 'seq', split_axis=1, concat_axis=0, tiled...  5.46 us
    all_to_all x1, starting transfers between devices, local(): lax.all_to_all(local_total[None], 'seq', split_axis=1, concat_axis=0, til...  5.09 us
    all_to_all x1, starting transfers between devices, local(): lax.all_to_all(local_top[None], 'seq', split_axis=1, concat_axis=0, tiled...  4.74 us
  transfers between devices with their start and end apart: 3, of which 2 were waited for; matrix products, arithmetic and copies ran while one was open for 13% of the time, Pallas kernels for 0%

commit v1 on v0

--- a/solution.py
+++ b/solution.py
@@ -13,7 +13,16 @@
     block_len = key_cache.shape[1]
     seq_count = lengths.shape[0]
     scale = 1.0 / math.sqrt(head_size)
-    whole_query = lax.all_gather(query, "seq", axis=0, tiled=True)
+    ways = lax.axis_size("seq")
+    up = [(d, (d + 1) % ways) for d in range(ways)]
+    down = [(d, (d - 1) % ways) for d in range(ways)]
+    earlier, later = ([query], [query])
+    for _ in range(ways // 2):
+        earlier.append(lax.ppermute(earlier[-1], "seq", up))
+    for _ in range((ways - 1) // 2):
+        later.append(lax.ppermute(later[-1], "seq", down))
+    line = jnp.concatenate([*earlier[::-1], *later[1:]], axis=0)
+    whole_query = jnp.roll(line, (lax.axis_index("seq") - ways // 2) * query.shape[0], axis=0)
     query_rows = jnp.take(whole_query, block_seq, axis=0).reshape(blocks_here, heads, head_size)
     keys = key_cache.reshape(blocks_here, block_len, heads, head_size)
     values = value_cache.reshape(blocks_here, block_len, heads, head_size)

time: 96.1 us -> 87.6 us (0.912)
  blocking collectives: 39.5 us -> 24.4 us
  starting transfers between devices: 13.1 us -> 16.9 us
  waiting for transfers between devices: 9.12 us -> 11.7 us
    all_gather x1 -> x0, blocking collectives: 15.1 us -> none  [local(): whole_query = lax.all_gather(query, 'seq', axis=0, tiled=True)]
    ppermute x0 -> x3, starting transfers between devices: none -> 5.14 us  [the longest x2 3.05 us: local(): earlier.append(lax.ppermute(earlier[-1], 'seq', up))]
    all_to_all x1, starting transfers between devices: 5.09 us -> 3.4 us  [local(): lax.all_to_all(local_total[None], 'seq', split_axis=1, concat_axis=0, til...]
    all_to_all x1, waiting for transfers between devices: 0.01 us -> 1.7 us  [local(): lax.all_to_all(local_top[None], 'seq', split_axis=1, concat_axis=0, tiled...]
    unnamed x11 -> x12, local copies, waits for them, and re-layouts: 12.6 us -> 12.6 us
  transfers between devices with their start and end apart: 3 -> 6, of which waited for: 2 -> 3; matrix products, arithmetic and copies ran while one was open for 13% -> 24% of each run, Pallas kernels for 0% -> 0%
where the time goes in v1:
time: 87.6 us; the launch traced here: 86.8 us
  blocking collectives  24.4 us (28%)
  starting transfers between devices  16.9 us (19%)
  local copies, waits for them, and re-layouts  16.8 us (19%)
  matrix products  12.5 us (14%)
  waiting for transfers between devices  11.7 us (13%)
  other arithmetic  3.76 us (4%)
    all_gather x1, blocking collectives, local(): attention = lax.all_gather(mine, 'seq', axis=0, tiled=True)  13.2 us
    unnamed x12, local copies, waits for them, and re-layouts  12.6 us
    unnamed x1, blocking collectives  11.3 us
    dot_general x1, matrix products, local(): jnp.dot(attention, out_weight, preferred_element_type=jnp.float32)  6.41 us
    all_to_all x1, waiting for transfers between devices, local(): lax.all_to_all(local_acc[None], 'seq', split_axis=1, concat_axis=0, tiled...  5.46 us
    all_to_all x1, starting transfers between devices, local(): lax.all_to_all(local_top[None], 'seq', split_axis=1, concat_axis=0, tiled...  5.08 us
    all_to_all x1, waiting for transfers between devices, local(): lax.all_to_all(local_total[None], 'seq', split_axis=1, concat_axis=0, til...  4.5 us
    all_to_all x1, starting transfers between devices, local(): lax.all_to_all(local_total[None], 'seq', split_axis=1, concat_axis=0, til...  3.4 us
  transfers between devices with their start and end apart: 6, of which 3 were waited for; matrix products, arithmetic and copies ran while one was open for 24% of the time, Pallas kernels for 0%

profile of v1, /device:TPU:0, one launch (start us, length us, event | category | flops | bytes accessed | tf_op | source)
XLA Modules:
  0.0 86.8 jit_solution(4952878045545377944)
XLA Ops:
  0.0 0.0 copy-start
  0.0 3.1 %collective-permute-start = (bf16[2,1792]{1,0:T(2,128)(2,1)}, bf16[2,1792]{1,0:T(2,128)(2,1)S(1)}, u32[]{:S(2)}, u32[]{:S(2)}) collective-permute-start(bf16[2,1792]{1,0:T(2,128)(2,1)} %param.8), channel_id=1, source_target_pairs={{0,4},{4,8},{8,12},{12,0},{1,5},{5,9},{9,13},{13,1},{2,6},{6,10},{... | collective-permute-start | bytes 21512 | tf_op jit(solution)/shard_map/ppermute | solution.py:21
  3.1 2.1 %collective-permute-start.2 = (bf16[2,1792]{1,0:T(2,128)(2,1)}, bf16[2,1792]{1,0:T(2,128)(2,1)S(1)}, u32[]{:S(2)}, u32[]{:S(2)}) collective-permute-start(bf16[2,1792]{1,0:T(2,128)(2,1)} %param.8), channel_id=1, source_target_pairs={{0,12},{4,0},{8,4},{12,8},{1,13},{5,1},{9,5},{13,9},{2,14},{6,2},{... | collective-permute-start | bytes 21512 | tf_op jit(solution)/shard_map/ppermute | solution.py:23
  5.1 0.7 compare_select_fusion
  5.8 0.0 copy-done
  5.8 0.6 gather_fusion
  6.4 0.7 broadcast_add_fusion
  7.1 0.1 fusion.16
  7.2 0.1 subtract_convert_fusion
  7.3 0.7 compare_and_fusion
  7.9 0.0 collective-permute-done
  7.9 0.0 collective-permute-start.1
  7.9 0.7 iota_compare_fusion
  8.7 6.0 %copy.49 = bf16[4,256,1792]{1,2,0:T(8,128)(2,1)} copy(bf16[4,256,1792]{2,1,0:T(8,128)(2,1)} %param.9) | data formatting | bytes 7340032 | tf_op args[1]
  14.7 6.0 %copy.50 = bf16[4,256,1792]{1,2,0:T(8,128)(2,1)} copy(bf16[4,256,1792]{2,1,0:T(8,128)(2,1)} %param.10) | data formatting | bytes 7340032 | tf_op args[2]
  20.6 0.0 copy-done.3
  20.7 0.6 dynamic-slice
  21.9 0.0 collective-permute-done.2
  21.9 0.0 collective-permute-done.1
  21.9 0.0 copy-done.1
  21.9 0.1 concatenate.6
  22.1 0.6 gather_fusion.1
  22.7 0.1 select_bitcast_fusion
  22.7 2.6 %fusion.9 = f32[4,14,1,256]{3,2,1,0:T(1,128)S(1)} fusion(bf16[4,256,14,128]{1,3,2,0:T(8,128)(2,1)} %bitcast.33, bf16[4,14,128,1]{2,1,0,3:T(8,128)(2,1)S(1)} %select_bitcast_fusion), kind=kOutput, calls=%fused_computation.16 | convolution fusion | flops 3670016 | bytes 3741696 | tf_op jit(solution)/shard_map/bthd,bhd->bht/dot_general | solution.py:30
  25.3 0.0 copy-done.2
  25.3 0.2 fusion.18
  25.5 0.2 fusion.4
  25.7 0.1 select_reduce_fusion
  25.8 0.7 copy.54
  26.5 5.1 %all-to-all-start.1 = ((f32[1,8,14]{2,0,1:T(1,128)}), f32[1,8,14]{2,0,1:T(1,128)S(1)}, u32[]{:S(2)}, u32[]{:S(2)}) async-start(f32[1,8,14]{2,0,1:T(1,128)} %copy.54), calls=%async_computation.1 | async-start | bytes 8192 | tf_op jit(solution)/shard_map/all_to_all | solution.py:51
  31.6 3.1 %fusion.2 = f32[4,14,1,128]{3,2,1,0:T(1,128)S(1)} fusion(bf16[4,256,14,128]{1,3,2,0:T(8,128)(2,1)} %bitcast.32, bf16[4,14,256,1]{2,0,1,3:T(4,128)(2,1)S(1)} %get-tuple-element.10), kind=kOutput, calls=%fused_computation.6 | convolution fusion | flops 3670016 | bytes 3727360 | tf_op jit(solution)/shard_map/bht,bthd->bhd/dot_general | solution.py:41
  34.6 0.1 multiply_reduce_fusion.1
  34.8 0.7 copy.57
  35.4 1.7 %all-to-all-done.1 = f32[1,8,14]{2,0,1:T(1,128)S(1)} async-done(((f32[1,8,14]{2,0,1:T(1,128)}), f32[1,8,14]{2,0,1:T(1,128)S(1)}, u32[]{:S(2)}, u32[]{:S(2)}) %all-to-all-start.1) | async-done | bytes 480 | tf_op jit(solution)/shard_map/all_to_all | solution.py:51
  37.1 3.4 %all-to-all-start.2 = ((f32[1,8,14]{2,0,1:T(1,128)}), f32[1,8,14]{2,0,1:T(1,128)S(1)}, u32[]{:S(2)}, u32[]{:S(2)}) async-start(f32[1,8,14]{2,0,1:T(1,128)} %copy.57), calls=%async_computation.2 | async-start | bytes 8192 | tf_op jit(solution)/shard_map/all_to_all | solution.py:52
  40.5 0.4 convolution_bitcast_fusion
  40.9 0.7 copy.51
  41.6 4.5 %all-to-all-done.2 = f32[1,8,14]{2,0,1:T(1,128)S(1)} async-done(((f32[1,8,14]{2,0,1:T(1,128)}), f32[1,8,14]{2,0,1:T(1,128)S(1)}, u32[]{:S(2)}, u32[]{:S(2)}) %all-to-all-start.2) | async-done | bytes 480 | tf_op jit(solution)/shard_map/all_to_all | solution.py:52
  46.1 3.3 %all-to-all-start = ((f32[1,8,14,128]{3,0,2,1:T(1,128)}), f32[1,8,14,128]{3,0,2,1:T(1,128)S(1)}, u32[]{:S(2)}, u32[]{:S(2)}) async-start(f32[1,8,14,128]{3,0,2,1:T(1,128)} %copy.51), calls=%async_computation | async-start | bytes 114688 | tf_op jit(solution)/shard_map/all_to_all | solution.py:53
  49.4 0.1 copy.55
  49.5 0.1 copy.58
  49.6 5.5 %all-to-all-done = f32[1,8,14,128]{3,0,2,1:T(1,128)S(1)} async-done(((f32[1,8,14,128]{3,0,2,1:T(1,128)}), f32[1,8,14,128]{3,0,2,1:T(1,128)S(1)}, u32[]{:S(2)}, u32[]{:S(2)}) %all-to-all-start) | async-done | bytes 57376 | tf_op jit(solution)/shard_map/all_to_all | solution.py:53
  55.1 0.1 multiply_reduce_fusion
  55.2 0.1 fusion.15
  55.3 13.2 %all-gather = bf16[4,2,1792]{2,1,0:T(2,128)(2,1)S(1)} all-gather(bf16[1,2,1792]{2,1,0:T(2,128)(2,1)S(1)} %fusion.15), channel_id=1, replica_groups=mesh['group'=2,'seq'=4,'tensor'=4] {'seq'}, dimensions={0}, use_global_device_ids=true | all-gather | bytes 35840 | tf_op jit(solution)/shard_map/all_gather | solution.py:64
  68.5 6.4 %fusion.20 = f32[8,3584]{1,0:T(8,128)S(1)} fusion(bf16[8,1792]{1,0:T(8,128)(2,1)S(1)} %reshape.150, bf16[1792,3584]{1,0:T(8,128)(2,1)} %param.15), kind=kOutput, calls=%fused_computation.42 | convolution fusion | flops 102760448 | bytes 12988416 | tf_op jit(solution)/shard_map/dot_general | solution.py:66
  74.9 11.3 %all-reduce = bf16[8,3584]{1,0:T(8,128)(2,1)S(1)} all-reduce(f32[8,3584]{1,0:T(8,128)S(1)} %fusion.20), channel_id=2, replica_groups=mesh['group'=2,'seq'=4,'tensor'=4] {'tensor'}, use_global_device_ids=true, to_apply=%region_7.8.clone | all-reduce | flops 28672 | bytes 172032
  86.2 0.6 dynamic-slice_convert_fusion
  (10 shorter events, 0.1 us)
Async XLA Ops:
  0.0 5.8 %copy-start = (s32[8]{0:T(128)S(1)}, s32[8]{0:T(128)}, u32[]{:S(2)}) copy-start(s32[8]{0:T(128)} %param.14) | copy-start | bytes 100
  0.0 7.9 %collective-permute-start = (bf16[2,1792]{1,0:T(2,128)(2,1)}, bf16[2,1792]{1,0:T(2,128)(2,1)S(1)}, u32[]{:S(2)}, u32[]{:S(2)}) collective-permute-start(bf16[2,1792]{1,0:T(2,128)(2,1)} %param.8), channel_id=1, source_target_pairs={{0,4},{4,8},{8,12},{12,0},{1,5},{5,9},{9,13},{13,1},{2,6},{6,10},{... | collective-permute-start | bytes 21512 | tf_op jit(solution)/shard_map/ppermute | solution.py:21
  3.1 18.8 %collective-permute-start.2 = (bf16[2,1792]{1,0:T(2,128)(2,1)}, bf16[2,1792]{1,0:T(2,128)(2,1)S(1)}, u32[]{:S(2)}, u32[]{:S(2)}) collective-permute-start(bf16[2,1792]{1,0:T(2,128)(2,1)} %param.8), channel_id=1, source_target_pairs={{0,12},{4,0},{8,4},{12,8},{1,13},{5,1},{9,5},{13,9},{2,14},{6,2},{... | collective-permute-start | bytes 21512 | tf_op jit(solution)/shard_map/ppermute | solution.py:23
  7.9 14.0 %collective-permute-start.1 = (bf16[2,1792]{1,0:T(2,128)(2,1)S(1)}, bf16[2,1792]{1,0:T(2,128)(2,1)S(1)}, u32[]{:S(2)}, u32[]{:S(2)}) collective-permute-start(bf16[2,1792]{1,0:T(2,128)(2,1)S(1)} %collective-permute-done), channel_id=1, source_target_pairs={{0,4},{4,8},{8,12},{12,0},{1,5},{5,9},{9,13},{13,1},{2,6},{6,10},{... | collective-permute-start | bytes 21512 | tf_op jit(solution)/shard_map/ppermute | solution.py:21
  14.7 6.0 %copy-start.3 = (u32[32]{0:T(128)S(1)}, u32[32]{0:T(128)}, u32[]{:S(2)}) copy-start(u32[32]{0:T(128)} %constant.67) | copy-start | bytes 388
  14.7 7.2 %copy-start.1 = (bf16[2,1792]{1,0:T(2,128)(2,1)S(1)}, bf16[2,1792]{1,0:T(2,128)(2,1)}, u32[]{:S(2)}) copy-start(bf16[2,1792]{1,0:T(2,128)(2,1)} %param.8) | copy-start | bytes 21508
  20.6 4.7 %copy-start.2 = (f32[14]{0:T(128)S(1)}, f32[14]{0:T(128)}, u32[]{:S(2)}) copy-start(f32[14]{0:T(128)} %param.11) | copy-start | bytes 172
  26.5 10.7 %all-to-all-start.1 = ((f32[1,8,14]{2,0,1:T(1,128)}), f32[1,8,14]{2,0,1:T(1,128)S(1)}, u32[]{:S(2)}, u32[]{:S(2)}) async-start(f32[1,8,14]{2,0,1:T(1,128)} %copy.54), calls=%async_computation.1 | async-start | bytes 8192 | tf_op jit(solution)/shard_map/all_to_all | solution.py:51
  37.1 9.0 %all-to-all-start.2 = ((f32[1,8,14]{2,0,1:T(1,128)}), f32[1,8,14]{2,0,1:T(1,128)S(1)}, u32[]{:S(2)}, u32[]{:S(2)}) async-start(f32[1,8,14]{2,0,1:T(1,128)} %copy.57), calls=%async_computation.2 | async-start | bytes 8192 | tf_op jit(solution)/shard_map/all_to_all | solution.py:52
  46.1 9.0 %all-to-all-start = ((f32[1,8,14,128]{3,0,2,1:T(1,128)}), f32[1,8,14,128]{3,0,2,1:T(1,128)S(1)}, u32[]{:S(2)}, u32[]{:S(2)}) async-start(f32[1,8,14,128]{3,0,2,1:T(1,128)} %copy.51), calls=%async_computation | async-start | bytes 114688 | tf_op jit(solution)/shard_map/all_to_all | solution.py:53
